TPU v7x, 8 devices: a whole 2x2x1 slice. The times are simulated.
8 devices in a mesh: side: 2 (over z, y), rep: 4 (over x, core).
Axes of the slice: x: 2, y: 2, z: 1, core: 2. Of those that a mesh axis runs over, the one named last changes fastest.
Arguments:
- w_up: float32 [2, 2, 2048, 6144], P('side', None, 'rep')
- w_down: float32 [2, 2, 6144, 2048], P('side', None, None, 'rep')
- g_up: float32 [2, 2, 2048, 6144], P('side', None, 'rep')
- g_down: float32 [2, 2, 6144, 2048], P('side', None, None, 'rep')
- learn_rate: float32 [], replicated
- prompts: bfloat16 [2, 16384, 2048], P('side', 'rep')
- prompt_lens: int32 [4], P('rep')
Outputs:
- output 1: float32 [2, 2, 2048, 6144], P('side', None, 'rep')
- output 2: float32 [2, 2, 6144, 2048], P('side', None, None, 'rep')
- output 3: bfloat16 [2, 16384, 2048], P('side', 'rep')
All inputs are finite; a program needn't handle non-finite values.
Results may differ from a plain program's by a relative error of at most 0.00783483.
Values are sent between devices in bfloat16 or wider.
A program may use at most 1 GiB of HBM per device.

v0:
```python
import jax
import jax.numpy as jnp
from jax import lax
from jax.sharding import PartitionSpec as P


def solution(mesh):
    side_devs = mesh.shape["side"]
    tp_ways = side_devs // 2
    cross_perm = [(src_pos, src_pos + tp_ways) for src_pos in range(tp_ways)]
    up_spec = P("side", None, "rep", None)
    down_spec = P("side", None, None, "rep")
    act_spec = P("side", "rep", None)

    def device_step(w_up, w_down, g_up, g_down, learn_rate, prompts, prompt_lens):
        new_up = w_up - learn_rate * g_up
        new_down = w_down - learn_rate * g_down
        up_sent = lax.ppermute(new_up[0].astype(jnp.bfloat16), "side", cross_perm)
        down_sent = lax.ppermute(new_down[0].astype(jnp.bfloat16), "side", cross_perm)
        up_full = lax.all_gather(up_sent, "rep", axis=1, tiled=True)
        down_full = lax.all_gather(down_sent, "rep", axis=2, tiled=True)
        side_idx = lax.axis_index("side")
        is_gen = side_idx >= tp_ways
        tokens = prompts.shape[1]
        d_piece = prompts.shape[2]
        if tp_ways > 1:
            pieces = lax.all_gather(prompts[0], "side", axis=0)
            hidden = jnp.transpose(pieces[tp_ways:], (1, 0, 2)).reshape(tokens, tp_ways * d_piece)
        else:
            hidden = prompts[0]
        for layer_idx in range(up_full.shape[0]):
            pre_act = jnp.dot(hidden, up_full[layer_idx], preferred_element_type=jnp.float32)
            act_bf = jax.nn.gelu(pre_act, approximate=True).astype(jnp.bfloat16)
            part_sum = jnp.dot(act_bf, down_full[layer_idx], preferred_element_type=jnp.float32)
            if tp_ways > 1:
                part_sum = lax.psum(jnp.where(is_gen, part_sum, 0.0), "side")
            hidden = (hidden.astype(jnp.float32) + part_sum).astype(jnp.bfloat16)
        keep_mask = jnp.arange(tokens)[:, None] < prompt_lens[0]
        tp_idx = jnp.maximum(side_idx - tp_ways, 0)
        own_cols = lax.dynamic_slice_in_dim(hidden, tp_idx * d_piece, d_piece, axis=1)
        out_block = jnp.where(keep_mask & is_gen, own_cols, jnp.zeros_like(own_cols))
        return new_up, new_down, out_block[None]

    mapped = jax.shard_map(
        device_step,
        mesh=mesh,
        in_specs=(up_spec, down_spec, up_spec, down_spec, P(), act_spec, P("rep")),
        out_specs=(up_spec, down_spec, act_spec),
        check_vma=False,
    )
    return mapped
```

profile of v0, /device:TPU:4, one launch (start us, length us, event | category | flops | bytes accessed | tf_op | source)
XLA Modules:
  0.0 1284.8 jit_solution(9341668722139431871)
XLA Ops:
  7.2 0.0 all-gather.3.cloned.1.call-start
  7.9 25.3 %convert_bitcast_fusion.1 = (bf16[2,512,6144]{2,1,0:T(8,128)(2,1)S(1)}, f32[1,2,512,6144]{3,2,1,0:T(8,128)}) fusion(f32[1,2,512,6144]{3,2,1,0:T(8,128)} %param.7, f32[1,2,512,6144]{3,2,1,0:T(8,128)} %param.9, f32[]{:T(128)S(6)} %copy.16), kind=kLoop, calls=%fused_computation.33 | loop fusion | flops 18874368 | bytes 88080384 | tf_op jit(solution)/shard_map/convert_element_type | solution.py:18
  33.1 1.3 collective-permute-start
  34.4 272.7 %collective-permute-done = bf16[2,512,6144]{2,1,0:T(8,128)(2,1)} collective-permute-done((bf16[2,512,6144]{2,1,0:T(8,128)(2,1)S(1)}, bf16[2,512,6144]{2,1,0:T(8,128)(2,1)}, u32[]{:S(2)}, u32[]{:S(2)}) %collective-permute-start) | collective-permute-done | bytes 12582944 | tf_op jit(solution)/shard_map/ppermute | solution.py:18
  307.1 0.0 all-gather.3.cloned.1.call-update
  307.1 0.0 all-gather.5.cloned.1.call-start
  307.2 25.3 %convert_bitcast_fusion = (bf16[2,6144,512]{2,1,0:T(8,128)(2,1)S(1)}, f32[1,2,6144,512]{3,2,1,0:T(8,128)}) fusion(f32[1,2,6144,512]{3,2,1,0:T(8,128)} %param.8, f32[1,2,6144,512]{3,2,1,0:T(8,128)} %param.10, f32[]{:T(128)S(6)} %copy.16), kind=kLoop, calls=%fused_computation.32 | loop fusion | flops 18874368 | bytes 88080384 | tf_op jit(solution)/shard_map/convert_element_type | solution.py:19
  332.5 1.5 collective-permute-start.1
  333.9 271.7 %collective-permute-done.1 = bf16[2,6144,512]{2,1,0:T(8,128)(2,1)} collective-permute-done((bf16[2,6144,512]{2,1,0:T(8,128)(2,1)S(1)}, bf16[2,6144,512]{2,1,0:T(8,128)(2,1)}, u32[]{:S(2)}, u32[]{:S(2)}) %collective-permute-start.1) | collective-permute-done | bytes 12582944 | tf_op jit(solution)/shard_map/ppermute | solution.py:19
  605.7 0.0 all-gather.5.cloned.1.call-update
  606.4 0.6 fusion.28
  607.0 0.0 all-gather.3.cloned.1.call-done
  607.0 134.3 %fusion.7 = bf16[4096,6144]{0,1:T(8,128)(2,1)} fusion(bf16[2,2048,6144]{2,1,0:T(8,128)(2,1)} %all-gather.3.cloned.1.call-done, bf16[1,4096,2048]{2,1,0:T(8,128)(2,1)} %param.12), kind=kOutput, calls=%fused_computation.9 | convolution fusion | flops 103305707520 | bytes 92274688 | tf_op jit(solution)/shard_map/dot_general | solution.py:32
  741.3 160.0 %all-gather.5.cloned.1.call-done = bf16[2,6144,2048]{2,1,0:T(8,128)(2,1)} async-done(((bf16[2,6144,512]{2,1,0:T(8,128)(2,1)}), bf16[2,6144,2048]{2,1,0:T(8,128)(2,1)}) %all-gather.5.cloned.1.call-update) | async-done | bytes 50331664 | tf_op jit(solution)/shard_map/all_gather | solution.py:21
  901.3 115.1 %fusion.20 = f32[4096,2048]{1,0:T(8,128)} fusion(bf16[4096,6144]{0,1:T(8,128)(2,1)} %fusion.7, bf16[2,6144,2048]{2,1,0:T(8,128)(2,1)} %all-gather.5.cloned.1.call-done), kind=kOutput, calls=%fused_computation.25 | convolution fusion | flops 103079215104 | bytes 109051904 | tf_op jit(solution)/shard_map/dot_general | solution.py:34
  1016.4 0.0 copy-start
  1016.4 144.4 %fusion.39 = bf16[4096,6144]{0,1:T(8,128)(2,1)} fusion(bf16[2,2048,6144]{2,1,0:T(8,128)(2,1)} %all-gather.3.cloned.1.call-done, f32[4096,2048]{1,0:T(8,128)} %fusion.20, bf16[1,4096,2048]{2,1,0:T(8,128)(2,1)} %param.12), kind=kOutput, calls=%fused_computation.17.clone.clone.clone.clone.clone.clone.2 | convolution fusion | flops 103330873344 | bytes 125829120 | tf_op jit(solution)/shard_map/dot_general | solution.py:32
  1160.8 0.0 copy-done
  1160.8 117.1 %select_bitcast_fusion = bf16[1,4096,2048]{2,1,0:T(8,128)(2,1)} fusion(pred[4096]{0:T(1024)(128)(4,1)S(1)} %copy-done, bf16[2,6144,2048]{2,1,0:T(8,128)(2,1)} %all-gather.5.cloned.1.call-done, f32[4096,2048]{1,0:T(8,128)} %fusion.20, bf16[1,4096,2048]{2,1,0:T(8,128)(2,1)} %param.12, bf16[4096,6144]{0,1:T(8,128)(2,1)} %fusion.39), kind=kOutput, calls=%fused_computation.31 | convolution fusion | flops 103137935360 | bytes 142610432 | tf_op jit(solution)/shard_map/dot_general | solution.py:34
Async XLA Ops:
  7.2 599.8 %all-gather.3.cloned.1.call-start = ((), (), s32[]{:S(2)}) async-start(), calls=%async_computation | async-start | bytes 62914560 | tf_op jit(solution)/shard_map/all_gather | solution.py:20
  33.1 274.0 %collective-permute-start = (bf16[2,512,6144]{2,1,0:T(8,128)(2,1)S(1)}, bf16[2,512,6144]{2,1,0:T(8,128)(2,1)}, u32[]{:S(2)}, u32[]{:S(2)}) collective-permute-start(bf16[2,512,6144]{2,1,0:T(8,128)(2,1)S(1)} %get-tuple-element.3), channel_id=1, source_target_pairs={{0,4},{1,5},{2,6},{3,7}} | collective-permute-start | bytes 37748744 | tf_op jit(solution)/shard_map/ppermute | solution.py:18
  307.1 594.2 %all-gather.5.cloned.1.call-start = ((), (), s32[]{:S(2)}) async-start(), calls=%async_computation.1 | async-start | bytes 62914560 | tf_op jit(solution)/shard_map/all_gather | solution.py:21
  332.5 273.2 %collective-permute-start.1 = (bf16[2,6144,512]{2,1,0:T(8,128)(2,1)S(1)}, bf16[2,6144,512]{2,1,0:T(8,128)(2,1)}, u32[]{:S(2)}, u32[]{:S(2)}) collective-permute-start(bf16[2,6144,512]{2,1,0:T(8,128)(2,1)S(1)} %get-tuple-element.5), channel_id=1, source_target_pairs={{0,4},{1,5},{2,6},{3,7}} | collective-permute-start | bytes 37748744 | tf_op jit(solution)/shard_map/ppermute | solution.py:19
  1016.4 144.4 %copy-start = (pred[4096]{0:T(1024)(128)(4,1)S(1)}, pred[4096]{0:T(1024)(128)(4,1)}, u32[]{:S(2)}) copy-start(pred[4096]{0:T(1024)(128)(4,1)} %fusion.28) | copy-start | bytes 12292
Sparse Core Ops, SparseCore 0:
  307.3 296.8 all-gather.2
  605.8 295.4 all-gather.4
where the time goes:
time: 1290 us; the launch traced here: 1280 us
  waiting for transfers between devices  704 us (55%)
  matrix products  511 us (40%)
  other arithmetic  51.2 us (4%)
  between operations  15.4 us (1%)
    dot_general x2, matrix products, device_step(): jnp.dot(hidden, up_full[layer_idx], preferred_element_type=jnp.float32)  279 us
    ppermute x1, waiting for transfers between devices, device_step(): up_sent = lax.ppermute(new_up[0].astype(jnp.bfloat16), 'side', cross_perm)  273 us
    ppermute x1, waiting for transfers between devices, device_step(): lax.ppermute(new_down[0].astype(jnp.bfloat16), 'side', cross_perm)  272 us
    dot_general x2, matrix products, device_step(): jnp.dot(act_bf, down_full[layer_idx], preferred_element_type=jnp.float32)  232 us
    all_gather x1, waiting for transfers between devices, device_step(): down_full = lax.all_gather(down_sent, 'rep', axis=2, tiled=True)  160 us
  transfers between devices with their start and end apart: 4, of which 3 were waited for; matrix products, arithmetic and copies ran while one was open for 12% of the time, Pallas kernels for 0%

commit v1 on v0

v1 whole, which is shorter than its diff:
```python
import jax
import jax.numpy as jnp
from jax import lax
from jax.experimental import pallas as pl
from jax.experimental.pallas import tpu as pltpu
from jax.sharding import PartitionSpec as P

MESH = pl.DeviceIdType.MESH
LAYERS, DIM, FFN, TOKENS = 2, 2048, 6144, 4096
RANKS = 4
COLS = DIM // RANKS
CHUNK = 512
CHUNKS = LAYERS * FFN // CHUNK
PER_LAYER = FFN // CHUNK
PARTS = 4
PART_ROWS = 2 * CHUNK // PARTS
PIECES = CHUNKS * PARTS
TILE = 512
TILES = TOKENS // TILE
STEPS = CHUNKS * TILES
AHEAD, X_LAG, PAIR_LAG = 12, 3, 1
PER = TILES // PARTS
WINDOW = 4
RING = 8


def update_kernel(lr_ref, w_up, g_up, w_dn, g_dn, new_up, new_dn, sent):
    lr = lr_ref[0]
    up = w_up[...] - lr * g_up[...]
    new_up[...] = up
    dn = w_dn[...] - lr * g_dn[...]
    new_dn[...] = dn
    half = PARTS // 2
    sent[0:half] = up.astype(jnp.bfloat16).reshape(half, PART_ROWS, CHUNK)
    sent[half:PARTS] = dn.astype(jnp.bfloat16).reshape(half, PART_ROWS, COLS)


def update(learn_rate, w_up, g_up, w_dn, g_dn):
    up_spec = pl.BlockSpec((None, None, COLS, CHUNK), lambda c: (0, c // PER_LAYER, 0, c % PER_LAYER))
    dn_spec = pl.BlockSpec((None, None, CHUNK, COLS), lambda c: (0, c // PER_LAYER, c % PER_LAYER, 0))
    return pl.pallas_call(
        update_kernel,
        grid=(CHUNKS,),
        out_shape=(
            jax.ShapeDtypeStruct(w_up.shape, jnp.float32),
            jax.ShapeDtypeStruct(w_dn.shape, jnp.float32),
            jax.ShapeDtypeStruct((PIECES, PART_ROWS, CHUNK), jnp.bfloat16),
        ),
        in_specs=[pl.BlockSpec(memory_space=pltpu.SMEM), up_spec, up_spec, dn_spec, dn_spec],
        out_specs=(up_spec, dn_spec, pl.BlockSpec((PARTS, PART_ROWS, CHUNK), lambda c: (c, 0, 0))),
        cost_estimate=pl.CostEstimate(flops=100_000_000, bytes_accessed=176_000_000, transcendentals=0),
        name="update",
    )(learn_rate.reshape(1), w_up, g_up, w_dn, g_dn)


def gelu(z):
    return 0.5 * z * (1.0 + jnp.tanh(0.7978845608 * (z + 0.044715 * (z * z * z))))


def stack_kernel(
    sent, x_ref, land, y_ref, h, acc, w,
    y_send, y_recv, x_send, x_recv, own_send, own_recv, far_send, far_recv, w_sem, x_sem, out_sem,
):
    side, rep = lax.axis_index("side"), lax.axis_index("rep")
    pair = rep + 1 - 2 * lax.rem(rep, 2)
    cross = lax.rem(rep + 2, RANKS)
    cross_pair = lax.rem(pair + 2, RANKS)
    is_gen = side == 1

    def remote(src, piece, slot, send, recv, to):
        return pltpu.make_async_remote_copy(
            src_ref=src, dst_ref=land.at[piece, slot], send_sem=send, recv_sem=recv,
            device_id=to, device_id_type=MESH,
        )

    def y_copy(p):
        return remote(sent.at[p], p, rep, y_send.at[lax.rem(p, WINDOW)], y_recv.at[p], (1, rep))

    def x_copy(p, slot):
        return remote(land.at[p, slot], p, slot, x_send.at[lax.rem(p, RING)], x_recv.at[p], (1, cross))

    def own_copy(p, slot):
        return remote(land.at[p, slot], p, slot, own_send.at[lax.rem(p, RING)], own_recv.at[p], (1, pair))

    def far_copy(p, slot):
        return remote(land.at[p, slot], p, slot, far_send.at[lax.rem(p, RING)], far_recv.at[p], (1, pair))

    def load(p):
        k = lax.rem(p, PARTS)
        s = lax.rem(p // PARTS, 2)
        return pltpu.make_async_copy(
            land.at[p], w.at[s, k // 2, :, lax.rem(k, 2)], w_sem.at[s, k]
        )

    barrier = pltpu.get_barrier_semaphore()

    @pl.when(side == 0)
    def trainer():
        pl.semaphore_signal(barrier, inc=1, device_id=(1, rep), device_id_type=MESH)
        pl.semaphore_wait(barrier, 1)

        def send(p, _):
            @pl.when(p >= WINDOW)
            def _():
                y_copy(p - WINDOW).wait_send()

            y_copy(p).start()
            return 0

        lax.fori_loop(0, PIECES, send, 0)

        def drain(p, _):
            y_copy(p).wait_send()
            return 0

        lax.fori_loop(PIECES - WINDOW, PIECES, drain, 0)

    @pl.when(is_gen)
    def generator():
        x_in = pltpu.make_async_copy(x_ref, h, x_sem)
        x_in.start()
        for to in ((0, rep), (1, pair), (1, cross)):
            pl.semaphore_signal(barrier, inc=1, device_id=to, device_id_type=MESH)
        pl.semaphore_wait(barrier, 3)

        def rows_of(i):
            return pl.ds(pl.multiple_of(i * TILE, TILE), TILE)

        def out_copy(i):
            return pltpu.make_async_copy(h.at[rows_of(i)], y_ref.at[rows_of(i)], out_sem.at[i])

        def event(s, lag, fn):
            q = s + AHEAD - lag
            p = q // PER
            pl.when((lax.rem(q + PER * PIECES, PER) == 0) & (p >= 0) & (p < PIECES))(lambda: fn(p))

        def on_y(p):
            y_copy(p).wait_recv()

            @pl.when(p >= RING)
            def _():
                x_copy(p - RING, rep).wait_send()
                own_copy(p - RING, rep).wait_send()

            x_copy(p, rep).start()
            own_copy(p, rep).start()

        def on_x(p):
            x_copy(p, cross).wait_recv()

            @pl.when(p >= RING)
            def _():
                far_copy(p - RING, cross).wait_send()

            far_copy(p, cross).start()

        def on_pair(p):
            own_copy(p, pair).wait_recv()
            far_copy(p, cross_pair).wait_recv()
            load(p).start()

        def compute(c, i):
            slot = lax.rem(c, 2)

            @pl.when(i == 0)
            def _():
                for k in range(PARTS):
                    load(c * PARTS + k).wait()

            half = TILE // 2
            first = pl.multiple_of(i * TILE, TILE)
            parts = [pl.ds(first + k * half, half) for k in range(2)]
            pre = [
                jnp.dot(h[rows, :], w[slot, 0].reshape(DIM, CHUNK), preferred_element_type=jnp.float32)
                for rows in parts
            ]
            act = [gelu(z).astype(jnp.bfloat16) for z in pre]
            for rows, u in zip(parts, act):
                for n in range(RANKS):
                    acc[rows, n * COLS:(n + 1) * COLS] += jnp.dot(
                        u, w[slot, 1, n].reshape(CHUNK, COLS), preferred_element_type=jnp.float32
                    )

            rows = rows_of(i)

            @pl.when(lax.rem(c, PER_LAYER) == PER_LAYER - 1)
            def _():
                h[rows, :] = acc[rows, :].astype(jnp.bfloat16)

                @pl.when(c < CHUNKS - 1)
                def _():
                    acc[rows, :] = h[rows, :].astype(jnp.float32)

                @pl.when(c == CHUNKS - 1)
                def _():
                    out_copy(i).start()

        def step(t, _):
            s = t - AHEAD
            event(s, 0, on_y)
            event(s, X_LAG, on_x)
            event(s, X_LAG + PAIR_LAG, on_pair)

            @pl.when((s < 0) & (s >= -TILES))
            def _():
                i = s + TILES

                @pl.when(i == 0)
                def _():
                    x_in.wait()

                acc[rows_of(i), :] = h[rows_of(i), :].astype(jnp.float32)

            @pl.when(s >= 0)
            def _():
                compute(s // TILES, lax.rem(s, TILES))

            return 0

        lax.fori_loop(0, AHEAD + STEPS, step, 0)

        def drain(p, _):
            x_copy(p, rep).wait_send()
            own_copy(p, rep).wait_send()
            far_copy(p, cross).wait_send()
            return 0

        lax.fori_loop(PIECES - RING, PIECES, drain, 0)
        for i in range(TILES):
            out_copy(i).wait()


def mlp_stack(sent, x):
    dma = pltpu.SemaphoreType.DMA
    return pl.pallas_call(
        stack_kernel,
        out_shape=(
            jax.ShapeDtypeStruct((PIECES, RANKS, PART_ROWS, CHUNK), jnp.bfloat16),
            jax.ShapeDtypeStruct((TOKENS, DIM), jnp.bfloat16),
        ),
        in_specs=[pl.BlockSpec(memory_space=pl.ANY)] * 2,
        out_specs=(pl.BlockSpec(memory_space=pl.ANY),) * 2,
        scratch_shapes=[
            pltpu.VMEM((TOKENS, DIM), jnp.bfloat16),
            pltpu.VMEM((TOKENS, DIM), jnp.float32),
            pltpu.VMEM((2, 2, RANKS, PARTS // 2, PART_ROWS, CHUNK), jnp.bfloat16),
            dma((WINDOW,)), dma((PIECES,)),
            dma((RING,)), dma((PIECES,)),
            dma((RING,)), dma((PIECES,)),
            dma((RING,)), dma((PIECES,)),
            dma((2, PARTS)), dma, dma((TILES,)),
        ],
        compiler_params=pltpu.CompilerParams(
            collective_id=0, has_side_effects=True, vmem_limit_bytes=67_043_328
        ),
        cost_estimate=pl.CostEstimate(flops=412_000_000_000, bytes_accessed=300_000_000, transcendentals=50_000_000),
        name="stack",
    )(sent, x)


def solution(mesh):
    up_spec = P("side", None, "rep", None)
    down_spec = P("side", None, None, "rep")
    act_spec = P("side", "rep", None)

    def device_step(w_up, w_down, g_up, g_down, learn_rate, prompts, prompt_lens):
        new_up, new_down, sent = update(learn_rate, w_up, g_up, w_down, g_down)
        _, y = mlp_stack(sent, prompts[0])
        keep = (jnp.arange(TOKENS)[:, None] < prompt_lens[0]) & (lax.axis_index("side") == 1)
        return new_up, new_down, jnp.where(keep, y, jnp.zeros_like(y))[None]

    return jax.shard_map(
        device_step,
        mesh=mesh,
        in_specs=(up_spec, down_spec, up_spec, down_spec, P(), act_spec, P("rep")),
        out_specs=(up_spec, down_spec, act_spec),
        check_vma=False,
    )
```

time: 1290 us -> 664 us (0.51)
  waiting for transfers between devices: 704 us -> 0 us
  Pallas kernels: 0 us -> 647 us
  matrix products: 511 us -> 0 us
  other arithmetic: 51.2 us -> 14.6 us
  between operations: 15.4 us -> 1.94 us
    pallas_call x0 -> x2, Pallas kernels: none -> 647 us  [the longest x1 588 us: mlp_stack(): pl.pallas_call(stack_kernel, out_shape=(jax.ShapeDtypeStruct((PIECES, RAN...]
    ppermute x2 -> x0, waiting for transfers between devices: 544 us -> none  [the longest x1 273 us: device_step(): up_sent = lax.ppermute(new_up[0].astype(jnp.bfloat16), 'side', cross_perm)]
    dot_general x4 -> x0, matrix products: 511 us -> none  [the longest x2 279 us: device_step(): jnp.dot(hidden, up_full[layer_idx], preferred_element_type=jnp.float32)]
    all_gather x2 -> x0, waiting for transfers between devices: 160 us -> none  [the longest x1 160 us: device_step(): down_full = lax.all_gather(down_sent, 'rep', axis=2, tiled=True)]
    convert_element_type x2 -> x0, other arithmetic: 50.6 us -> none  [the longest x1 25.3 us: device_step(): up_sent = lax.ppermute(new_up[0].astype(jnp.bfloat16), 'side', cross_perm)]
    broadcast_in_dim x0 -> x1, other arithmetic: none -> 14.6 us  [device_step(): return (new_up, new_down, jnp.where(keep, y, jnp.zeros_like(y))[None])]
  transfers between devices with their start and end apart: 4 -> 0, of which waited for: 3 -> 0; matrix products, arithmetic and copies ran while one was open for 12% -> 0% of each run, Pallas kernels for 0% -> 0%
where the time goes in v1:
time: 664 us; the launch traced here: 663 us
  Pallas kernels  647 us (97%)
  other arithmetic  14.6 us (2%)
    pallas_call x1, Pallas kernels, mlp_stack(): pl.pallas_call(stack_kernel, out_shape=(jax.ShapeDtypeStruct((PIECES, RAN...  588 us
    pallas_call x1, Pallas kernels, update(): pl.pallas_call(update_kernel, grid=(CHUNKS,), out_shape=(jax.ShapeDtypeSt...  58.5 us
    broadcast_in_dim x1, other arithmetic, device_step(): return (new_up, new_down, jnp.where(keep, y, jnp.zeros_like(y))[None])  14.6 us

profile of v1, /device:TPU:4, one launch (start us, length us, event | category | flops | bytes accessed | tf_op | source)
XLA Modules:
  0.0 663.4 jit_solution(14067716034585934614)
XLA Ops:
  1.3 58.5 %update.1 = (f32[1,2,512,6144]{3,2,1,0:T(8,128)}, f32[1,2,6144,512]{3,2,1,0:T(8,128)}, bf16[96,256,512]{2,1,0:T(8,128)(2,1)}) custom-call(f32[1]{0:T(128)} %bitcast.5.lr_ref, f32[1,2,512,6144]{3,2,1,0:T(8,128)} %w_up.1, f32[1,2,512,6144]{3,2,1,0:T(8,128)} %g_up.1, f32[1,2,6144,512]{3,2,1,0:T(8,128)} %w_dn.1, f32[1,2,6144,512]{3,2,1,0:T(8,128)} %g_dn.1), custom_call_target="tpu_custom_call" | custom-call | flops 100000000 | bytes 176000000 | tf_op jit(solution)/shard_map/update/pallas_call | solution.py:41
  59.8 588.4 %stack.1 = (bf16[96,4,256,512]{3,2,1,0:T(8,128)(2,1)}, bf16[4096,2048]{1,0:T(8,128)(2,1)}) custom-call(bf16[96,256,512]{2,1,0:T(8,128)(2,1)} %get-tuple-element.9.sent, bf16[4096,2048]{1,0:T(8,128)(2,1)} %bitcast.7), custom_call_target="tpu_custom_call" | custom-call | flops 411999993856 | bytes 300000000 | tf_op jit(solution)/shard_map/stack/pallas_call | solution.py:235
  648.8 14.6 %select_bitcast_fusion = bf16[1,4096,2048]{2,1,0:T(8,128)(2,1)} fusion(bf16[4096,2048]{1,0:T(8,128)(2,1)} %get-tuple-element.10, pred[4096]{0:T(1024)(128)(4,1)S(1)} %fusion), kind=kLoop, calls=%fused_computation | loop fusion | flops 8388608 | bytes 33558528 | tf_op jit(solution)/shard_map/broadcast_in_dim | solution.py:270
  (1 shorter events, 0.0 us)

commit v2 on v1

v2 whole, which is shorter than its diff:
```python
import jax
import jax.numpy as jnp
from jax import lax
from jax.experimental import pallas as pl
from jax.experimental.pallas import tpu as pltpu
from jax.sharding import PartitionSpec as P

MESH = pl.DeviceIdType.MESH
LAYERS, DIM, FFN, TOKENS = 2, 2048, 6144, 4096
RANKS = 4
COLS = DIM // RANKS
CHUNK = 512
CHUNKS = LAYERS * FFN // CHUNK
PER_LAYER = FFN // CHUNK
PARTS = 4
PART_ROWS = 2 * CHUNK // PARTS
PIECES = CHUNKS * PARTS
TILE = 512
TILES = TOKENS // TILE
LAST = CHUNKS - 1
STEPS = LAST * TILES
AHEAD, X_LAG, PAIR_LAG = 12, 3, 1
PER = TILES // PARTS
WINDOW = 4
RING = 8
STAGES = 3
HELD = 56
BACK = 8
HALF = TILE // 2
STACK_VMEM = 8_300_000


def gelu(z):
    return 0.5 * z * (1.0 + jnp.tanh(0.7978845608 * (z + 0.044715 * (z * z * z))))


def piece_of(up_ref, dn_ref, c, k):
    layer, col = c // PER_LAYER, lax.rem(c, PER_LAYER) * CHUNK
    if k < PARTS // 2:
        cols = pl.ds(pl.multiple_of(col, CHUNK), CHUNK)
        return up_ref.at[0, layer, pl.ds(k * PART_ROWS, PART_ROWS), cols]
    first = pl.multiple_of(col + (k - PARTS // 2) * PART_ROWS, PART_ROWS)
    return dn_ref.at[0, layer, pl.ds(first, PART_ROWS), :]


def held_piece(acc, c, k):
    return acc.at[pl.ds(pl.multiple_of(c * PART_ROWS, PART_ROWS), PART_ROWS), pl.ds(k * CHUNK, CHUNK)]


def stage(acc, s):
    first = pl.multiple_of((HELD + s) // PARTS * PART_ROWS, PART_ROWS)
    col = pl.multiple_of(lax.rem(s, PARTS) * CHUNK, CHUNK)
    return acc.at[pl.ds(first, PART_ROWS), pl.ds(col, CHUNK)]


def rows_of(i):
    return pl.ds(pl.multiple_of(i * TILE, TILE), TILE)


def up_act(h, w_up, i):
    first = pl.multiple_of(i * TILE, TILE)
    parts = [pl.ds(first + k * HALF, HALF) for k in range(2)]
    pre = [
        jnp.dot(h[rows, :], w_up.reshape(DIM, CHUNK), preferred_element_type=jnp.float32)
        for rows in parts
    ]
    return [(rows, gelu(z).astype(jnp.bfloat16)) for rows, z in zip(parts, pre)]


def stack_kernel(
    lr_ref, lens, w_up, g_up, w_dn, g_dn, x_ref, land, left, h, acc, w,
    y_send, y_recv, x_send, x_recv, own_send, own_recv, far_send, far_recv,
    w_sem, x_sem, w_in, g_in, left_sem,
):
    del lens
    side, rep = lax.axis_index("side"), lax.axis_index("rep")
    pair = rep + 1 - 2 * lax.rem(rep, 2)
    cross = lax.rem(rep + 2, RANKS)
    cross_pair = lax.rem(pair + 2, RANKS)

    def remote(src, piece, slot, send, recv, to):
        return pltpu.make_async_remote_copy(
            src_ref=src, dst_ref=land.at[piece, slot], send_sem=send, recv_sem=recv,
            device_id=to, device_id_type=MESH,
        )

    def y_copy(p):
        s = lax.rem(p, RING)
        src = w.at[0, s // 4, lax.rem(s, 4), 0]
        return remote(src, p, rep, y_send.at[lax.rem(p, WINDOW)], y_recv.at[p], (1, rep))

    def x_copy(p, slot):
        return remote(land.at[p, slot], p, slot, x_send.at[lax.rem(p, RING)], x_recv.at[p], (1, cross))

    def own_copy(p, slot):
        return remote(land.at[p, slot], p, slot, own_send.at[lax.rem(p, RING)], own_recv.at[p], (1, pair))

    def far_copy(p, slot):
        return remote(land.at[p, slot], p, slot, far_send.at[lax.rem(p, RING)], far_recv.at[p], (1, pair))

    def load(p):
        k = lax.rem(p, PARTS)
        s = lax.rem(p // PARTS, 2)
        return pltpu.make_async_copy(
            land.at[p], w.at[s, k // 2, :, lax.rem(k, 2)], w_sem.at[s, k]
        )

    barrier = pltpu.get_barrier_semaphore()

    @pl.when(side == 0)
    def trainer():
        def w_stage(s):
            return stage(acc, s)

        def g_stage(s):
            return stage(acc, PARTS + s)

        def fetch(c, k):
            s = lax.rem(c * PARTS + k, STAGES)
            return (
                pltpu.make_async_copy(piece_of(w_up, w_dn, c, k), w_stage(s), w_in.at[s]),
                pltpu.make_async_copy(piece_of(g_up, g_dn, c, k), g_stage(s), g_in.at[s]),
            )

        def spill(p):
            s = lax.rem(p, STAGES)
            return pltpu.make_async_copy(w_stage(s), left.at[p - HELD], left_sem.at[s])

        for k in range(2):
            for copy in fetch(0, k):
                copy.start()
        pl.semaphore_signal(barrier, inc=1, device_id=(1, rep), device_id_type=MESH)
        pl.semaphore_wait(barrier, 1)
        lr = lr_ref[0]

        def send(p):
            @pl.when(p >= WINDOW)
            def _():
                y_copy(p - WINDOW).wait_send()

            y_copy(p).start()

        def chunk(c, _):
            for k in range(PARTS):
                p = c * PARTS + k
                for copy in fetch(c, k):
                    copy.wait()
                s = lax.rem(p, STAGES)
                new = w_stage(s)[...] - lr * g_stage(s)[...]
                r = lax.rem(p, RING)
                w[0, r // 4, lax.rem(r, 4), 0] = new.astype(jnp.bfloat16)

                @pl.when(p < HELD)
                def _():
                    held_piece(acc, c, k)[...] = new

                @pl.when(p >= HELD)
                def _():
                    w_stage(s)[...] = new

                @pl.when(p >= 1)
                def _():
                    send(p - 1)

                @pl.when(p - 1 >= HELD)
                def _():
                    spill(p - 1).start()
                    spill(p - 1).wait()

                ahead = k + 2

                @pl.when(p + 2 < PIECES)
                def _():
                    for copy in fetch(c + ahead // PARTS, ahead % PARTS):
                        copy.start()

            return 0

        lax.fori_loop(0, CHUNKS, chunk, 0)
        send(PIECES - 1)
        spill(PIECES - 1).start()
        spill(PIECES - 1).wait()

        def drain(p, _):
            y_copy(p).wait_send()
            return 0

        lax.fori_loop(PIECES - WINDOW, PIECES, drain, 0)

    @pl.when(side == 1)
    def generator():
        x_in = pltpu.make_async_copy(x_ref, h, x_sem)
        x_in.start()
        for to in ((0, rep), (1, pair), (1, cross)):
            pl.semaphore_signal(barrier, inc=1, device_id=to, device_id_type=MESH)
        pl.semaphore_wait(barrier, 3)

        def event(s, lag, fn):
            q = s + AHEAD - lag
            p = q // PER
            pl.when((lax.rem(q + PER * PIECES, PER) == 0) & (p >= 0) & (p < PIECES))(lambda: fn(p))

        def on_y(p):
            y_copy(p).wait_recv()

            @pl.when(p >= RING)
            def _():
                x_copy(p - RING, rep).wait_send()
                own_copy(p - RING, rep).wait_send()

            x_copy(p, rep).start()
            own_copy(p, rep).start()

        def on_x(p):
            x_copy(p, cross).wait_recv()

            @pl.when(p >= RING)
            def _():
                far_copy(p - RING, cross).wait_send()

            far_copy(p, cross).start()

        def on_pair(p):
            own_copy(p, pair).wait_recv()
            far_copy(p, cross_pair).wait_recv()
            load(p).start()

        def compute(c, i):
            slot = lax.rem(c, 2)

            @pl.when(i == 0)
            def _():
                for k in range(PARTS):
                    load(c * PARTS + k).wait()

            for rows, u in up_act(h, w[slot, 0], i):
                for n in range(RANKS):
                    acc[rows, n * COLS:(n + 1) * COLS] += jnp.dot(
                        u, w[slot, 1, n].reshape(CHUNK, COLS), preferred_element_type=jnp.float32
                    )

            rows = rows_of(i)

            @pl.when(lax.rem(c, PER_LAYER) == PER_LAYER - 1)
            def _():
                h[rows, :] = acc[rows, :].astype(jnp.bfloat16)
                acc[rows, :] = h[rows, :].astype(jnp.float32)

        def step(t, _):
            s = t - AHEAD
            event(s, 0, on_y)
            event(s, X_LAG, on_x)
            event(s, X_LAG + PAIR_LAG, on_pair)

            @pl.when((s < 0) & (s >= -TILES))
            def _():
                i = s + TILES

                @pl.when(i == 0)
                def _():
                    x_in.wait()

                acc[rows_of(i), :] = h[rows_of(i), :].astype(jnp.float32)

            @pl.when(s >= 0)
            def _():
                compute(s // TILES, lax.rem(s, TILES))

            return 0

        lax.fori_loop(0, AHEAD + STEPS, step, 0)

        def drain(p, _):
            x_copy(p, rep).wait_send()
            own_copy(p, rep).wait_send()
            far_copy(p, cross).wait_send()
            return 0

        lax.fori_loop(PIECES - RING, PIECES, drain, 0)
        for k in range(PARTS):
            load(LAST * PARTS + k).wait()


def mlp_stack(lr, lens, w_up, g_up, w_dn, g_dn, x):
    dma = pltpu.SemaphoreType.DMA
    hbm = pl.BlockSpec(memory_space=pl.ANY)
    vmem = pl.BlockSpec(memory_space=pltpu.VMEM)
    return pl.pallas_call(
        stack_kernel,
        out_shape=(
            jax.ShapeDtypeStruct((PIECES, RANKS, PART_ROWS, CHUNK), jnp.bfloat16),
            jax.ShapeDtypeStruct((PIECES - HELD, PART_ROWS, CHUNK), jnp.float32),
            pltpu.VMEM((TOKENS, DIM), jnp.bfloat16),
            pltpu.VMEM((TOKENS, DIM), jnp.float32),
            pltpu.VMEM((2, 2, RANKS, PARTS // 2, PART_ROWS, CHUNK), jnp.bfloat16),
        ),
        in_specs=[pl.BlockSpec(memory_space=pltpu.SMEM)] * 2 + [hbm] * 5,
        out_specs=(hbm, hbm, vmem, vmem, vmem),
        scratch_shapes=[
            dma((WINDOW,)), dma((PIECES,)),
            dma((RING,)), dma((PIECES,)),
            dma((RING,)), dma((PIECES,)),
            dma((RING,)), dma((PIECES,)),
            dma((2, PARTS)), dma, dma((STAGES,)), dma((STAGES,)), dma((STAGES,)),
        ],
        compiler_params=pltpu.CompilerParams(
            collective_id=0, has_side_effects=True, vmem_limit_bytes=STACK_VMEM
        ),
        cost_estimate=pl.CostEstimate(flops=400_000_000_000, bytes_accessed=300_000_000, transcendentals=50_000_000),
        name="stack",
    )(lr, lens, w_up, g_up, w_dn, g_dn, x)


def last_kernel(
    lens, left, h_in, acc_in, w, new_up, new_dn, y_ref, h, acc, zero, zero_sem, held_sem, back_in, back_out, y_sem
):
    del h_in, acc_in
    side = lax.axis_index("side")

    def y_copy(slot, j):
        rows = pl.ds(pl.multiple_of(j * HALF, HALF), HALF)
        return pltpu.make_async_copy(
            h.at[pl.ds(pl.multiple_of(slot * HALF, HALF), HALF)], y_ref.at[0, rows], y_sem
        )

    @pl.when(side == 0)
    def trainer():
        def held_copy(c, k):
            return pltpu.make_async_copy(held_piece(acc, c, k), piece_of(new_up, new_dn, c, k), held_sem)

        def each(lo, hi, fn):
            def body(c, _):
                for k in range(PARTS):
                    fn(c, k)
                return 0

            lax.fori_loop(lo, hi, body, 0)

        def back_read(c, k):
            b = lax.rem(c, BACK // PARTS) * PARTS + k
            return pltpu.make_async_copy(left.at[c * PARTS + k - HELD], stage(acc, b), back_in.at[b])

        def back_write(c, k):
            b = lax.rem(c, BACK // PARTS) * PARTS + k
            return pltpu.make_async_copy(stage(acc, b), piece_of(new_up, new_dn, c, k), back_out.at[b])

        held = HELD // PARTS
        each(held, held + BACK // PARTS, lambda c, k: back_read(c, k).start())
        each(0, held, lambda c, k: held_copy(c, k).start())
        h[0:HALF, :] = jnp.zeros((HALF, DIM), jnp.bfloat16)

        def bring(c, _):
            for k in range(PARTS):
                back_read(c, k).wait()
                back_write(c, k).start()

            @pl.when((c > held) & (c + 1 < CHUNKS))
            def _():
                for k in range(PARTS):
                    back_write(c - 1, k).wait()
                    back_read(c + 1, k).start()

            return 0

        lax.fori_loop(held, CHUNKS, bring, 0)
        for j in range(2 * TILES):
            y_copy(0, j).start()
        each(0, held, lambda c, k: held_copy(c, k).wait())
        each(CHUNKS - 2, CHUNKS, lambda c, k: back_write(c, k).wait())
        for j in range(2 * TILES):
            y_copy(0, j).wait()

    @pl.when(side == 1)
    def generator():
        zero[...] = jnp.zeros_like(zero)

        def each_zero(fn):
            def body(c, _):
                for k in range(PARTS):
                    fn(pltpu.make_async_copy(zero, piece_of(new_up, new_dn, c, k), zero_sem))
                return 0

            lax.fori_loop(0, CHUNKS, body, 0)

        length = lens[0]
        slot = LAST % 2

        def step(i, _):
            for k, (rows, u) in enumerate(up_act(h, w[slot, 0], i)):
                j = 2 * i + k
                at = lax.broadcasted_iota(jnp.int32, (HALF, COLS), 0) + j * HALF
                for n in range(RANKS):
                    cols = slice(n * COLS, (n + 1) * COLS)
                    total = acc[rows, cols] + jnp.dot(
                        u, w[slot, 1, n].reshape(CHUNK, COLS), preferred_element_type=jnp.float32
                    )
                    h[rows, cols] = jnp.where(at < length, total, 0.0).astype(jnp.bfloat16)

            @pl.when(i == 0)
            def _():
                each_zero(lambda copy: copy.start())

            @pl.when(i >= 1)
            def _():
                y_copy(2 * i - 2, 2 * i - 2).start()
                y_copy(2 * i - 1, 2 * i - 1).start()

            return 0

        lax.fori_loop(0, TILES, step, 0)
        for j in range(2 * TILES - 2, 2 * TILES):
            y_copy(j, j).start()
        each_zero(lambda copy: copy.wait())
        for j in range(2 * TILES):
            y_copy(j, j).wait()


def last_step(lens, left, h, acc, w, up_shape, dn_shape, y_shape):
    dma = pltpu.SemaphoreType.DMA
    hbm = pl.BlockSpec(memory_space=pl.ANY)
    vmem = pl.BlockSpec(memory_space=pltpu.VMEM)
    h, acc, w = (pltpu.with_memory_space_constraint(v, pltpu.VMEM) for v in (h, acc, w))
    new_up, new_dn, y, _, _ = pl.pallas_call(
        last_kernel,
        out_shape=(
            jax.ShapeDtypeStruct(up_shape, jnp.float32),
            jax.ShapeDtypeStruct(dn_shape, jnp.float32),
            jax.ShapeDtypeStruct(y_shape, jnp.bfloat16),
            pltpu.VMEM((TOKENS, DIM), jnp.bfloat16),
            pltpu.VMEM((TOKENS, DIM), jnp.float32),
        ),
        in_specs=[pl.BlockSpec(memory_space=pltpu.SMEM), hbm, vmem, vmem, vmem],
        out_specs=(hbm, hbm, hbm, vmem, vmem),
        input_output_aliases={2: 3, 3: 4},
        scratch_shapes=[
            pltpu.VMEM((PART_ROWS, CHUNK), jnp.float32),
            dma, dma, dma((BACK,)), dma((BACK,)), dma,
        ],
        compiler_params=pltpu.CompilerParams(vmem_limit_bytes=STACK_VMEM),
        cost_estimate=pl.CostEstimate(flops=18_000_000_000, bytes_accessed=67_000_000, transcendentals=2_000_000),
        name="last",
    )(lens, left, h, acc, w)
    return new_up, new_dn, y


def solution(mesh):
    up_spec = P("side", None, "rep", None)
    down_spec = P("side", None, None, "rep")
    act_spec = P("side", "rep", None)

    def device_step(w_up, w_down, g_up, g_down, learn_rate, prompts, prompt_lens):
        _, left, h, acc, w = mlp_stack(
            learn_rate.reshape(1), prompt_lens, w_up, g_up, w_down, g_down, prompts[0]
        )
        return last_step(prompt_lens, left, h, acc, w, w_up.shape, w_down.shape, prompts.shape)

    return jax.shard_map(
        device_step,
        mesh=mesh,
        in_specs=(up_spec, down_spec, up_spec, down_spec, P(), act_spec, P("rep")),
        out_specs=(up_spec, down_spec, act_spec),
        check_vma=False,
    )
```

time: 664 us -> 591 us (0.89)
  Pallas kernels: 647 us -> 589 us
  other arithmetic: 14.6 us -> 0 us
    pallas_call x1, Pallas kernels: 58.5 us -> 23.8 us  [last_step(): pl.pallas_call(last_kernel, out_shape=(jax.ShapeDtypeStruct(up_shape, jnp...]
    pallas_call x1, Pallas kernels: 588 us -> 565 us  [mlp_stack(): pl.pallas_call(stack_kernel, out_shape=(jax.ShapeDtypeStruct((PIECES, RAN...]
    broadcast_in_dim x1 -> x0, other arithmetic: 14.6 us -> none  [device_step(): return (new_up, new_down, jnp.where(keep, y, jnp.zeros_like(y))[None])]
where the time goes in v2:
time: 591 us
  Pallas kernels  589 us (100%)
    pallas_call x1, Pallas kernels, mlp_stack(): pl.pallas_call(stack_kernel, out_shape=(jax.ShapeDtypeStruct((PIECES, RAN...  565 us
    pallas_call x1, Pallas kernels, last_step(): pl.pallas_call(last_kernel, out_shape=(jax.ShapeDtypeStruct(up_shape, jnp...  23.8 us

profile of v2, /device:TPU:4, one launch (start us, length us, event | category | flops | bytes accessed | tf_op | source)
XLA Modules:
  0.0 590.6 jit_solution(11880748781490241497)
XLA Ops:
  1.9 564.9 %stack.1 = (bf16[96,4,256,512]{3,2,1,0:T(8,128)(2,1)}, f32[40,256,512]{2,1,0:T(8,128)}, bf16[4096,2048]{1,0:T(8,128)(2,1)S(1)}, f32[4096,2048]{1,0:T(8,128)S(1)}, bf16[2,2,4,2,256,512]{5,4,3,2,1,0:T(8,128)(2,1)S(1)}) custom-call(f32[1]{0:T(128)} %bitcast.2.lr_ref, s32[1]{0:T(128)S(6)} %copy.15.lens, f32[1,2,512,6144]{3,2,1,0:T(8,128)} %w_up.1, ...), custom_call_target="tpu_custom_call" | custom-call | flops 399999991808 | bytes 300000000 | tf_op jit(solution)/shard_map/stack/pallas_call | solution.py:288
  566.8 23.8 %last.1 = (f32[1,2,512,6144]{3,2,1,0:T(8,128)}, f32[1,2,6144,512]{3,2,1,0:T(8,128)}, bf16[1,4096,2048]{2,1,0:T(8,128)(2,1)}, bf16[4096,2048]{1,0:T(8,128)(2,1)S(1)}, f32[4096,2048]{1,0:T(8,128)S(1)}) custom-call(s32[1]{0:T(128)S(6)} %copy.15.lens, f32[40,256,512]{2,1,0:T(8,128)} %get-tuple-element.10.left, ...), custom_call_target="tpu_custom_call", output_to_operand_aliasing={{3}: (2, {}), {4}: (3, {})} | custom-call | flops 17999998976 | bytes 67000000 | tf_op jit(solution)/shard_map/last/pallas_call | solution.py:423

commit v3 on v2

--- a/solution.py
+++ b/solution.py
@@ -15,18 +15,21 @@
 PARTS = 4
 PART_ROWS = 2 * CHUNK // PARTS
 PIECES = CHUNKS * PARTS
-TILE = 512
+BLOCK = 256
+TILE = 1024
 TILES = TOKENS // TILE
+PHASE = TILES
 LAST = CHUNKS - 1
-STEPS = LAST * TILES
-AHEAD, X_LAG, PAIR_LAG = 12, 3, 1
-PER = TILES // PARTS
+STEPS = LAST * 2 * PHASE + PHASE
+AHEAD, X_LAG, PAIR_LAG = 7, 3, 1
+PER = 2 * PHASE // PARTS
 WINDOW = 4
 RING = 8
 STAGES = 3
 HELD = 56
 BACK = 8
-HALF = TILE // 2
+OUT_TILE = 512
+UP_BLOCKS, DOWN_BLOCKS = 4, 4
 STACK_VMEM = 8_300_000
 
 
@@ -53,22 +56,20 @@
     return acc.at[pl.ds(first, PART_ROWS), pl.ds(col, CHUNK)]
 
 
-def rows_of(i):
-    return pl.ds(pl.multiple_of(i * TILE, TILE), TILE)
-
-
-def up_act(h, w_up, i):
-    first = pl.multiple_of(i * TILE, TILE)
-    parts = [pl.ds(first + k * HALF, HALF) for k in range(2)]
-    pre = [
-        jnp.dot(h[rows, :], w_up.reshape(DIM, CHUNK), preferred_element_type=jnp.float32)
-        for rows in parts
-    ]
-    return [(rows, gelu(z).astype(jnp.bfloat16)) for rows, z in zip(parts, pre)]
+def block_rows(b):
+    return pl.ds(pl.multiple_of(b * BLOCK, BLOCK), BLOCK)
+
+
+def down_cols(n):
+    return slice(n * COLS, (n + 1) * COLS)
+
+
+def down(u, wd, b, n):
+    return jnp.dot(u[b], wd[n].reshape(CHUNK, COLS), preferred_element_type=jnp.float32)
 
 
 def stack_kernel(
-    lr_ref, lens, w_up, g_up, w_dn, g_dn, x_ref, land, left, h, acc, w,
+    lr_ref, lens, w_up, g_up, w_dn, g_dn, x_ref, land, left, h, acc, u, wu, wd,
     y_send, y_recv, x_send, x_recv, own_send, own_recv, far_send, far_recv,
     w_sem, x_sem, w_in, g_in, left_sem,
 ):
@@ -85,9 +86,7 @@
         )
 
     def y_copy(p):
-        s = lax.rem(p, RING)
-        src = w.at[0, s // 4, lax.rem(s, 4), 0]
-        return remote(src, p, rep, y_send.at[lax.rem(p, WINDOW)], y_recv.at[p], (1, rep))
+        return remote(u.at[lax.rem(p, RING)], p, rep, y_send.at[lax.rem(p, WINDOW)], y_recv.at[p], (1, rep))
 
     def x_copy(p, slot):
         return remote(land.at[p, slot], p, slot, x_send.at[lax.rem(p, RING)], x_recv.at[p], (1, cross))
@@ -98,12 +97,10 @@
     def far_copy(p, slot):
         return remote(land.at[p, slot], p, slot, far_send.at[lax.rem(p, RING)], far_recv.at[p], (1, pair))
 
-    def load(p):
-        k = lax.rem(p, PARTS)
-        s = lax.rem(p // PARTS, 2)
-        return pltpu.make_async_copy(
-            land.at[p], w.at[s, k // 2, :, lax.rem(k, 2)], w_sem.at[s, k]
-        )
+    def load(p, k):
+        half = PARTS // 2
+        to = wu.at[:, k] if k < half else wd.at[:, k - half]
+        return pltpu.make_async_copy(land.at[p], to, w_sem.at[k])
 
     barrier = pltpu.get_barrier_semaphore()
 
@@ -147,8 +144,7 @@
                     copy.wait()
                 s = lax.rem(p, STAGES)
                 new = w_stage(s)[...] - lr * g_stage(s)[...]
-                r = lax.rem(p, RING)
-                w[0, r // 4, lax.rem(r, 4), 0] = new.astype(jnp.bfloat16)
+                u[lax.rem(p, RING)] = new.astype(jnp.bfloat16)
 
                 @pl.when(p < HELD)
                 def _():
@@ -223,28 +219,54 @@
         def on_pair(p):
             own_copy(p, pair).wait_recv()
             far_copy(p, cross_pair).wait_recv()
-            load(p).start()
-
-        def compute(c, i):
-            slot = lax.rem(c, 2)
-
+            for k in range(PARTS):
+                pl.when(lax.rem(p, PARTS) == k)(lambda k=k: load(p, k).start())
+
+        def up_phase(c, i):
             @pl.when(i == 0)
             def _():
-                for k in range(PARTS):
-                    load(c * PARTS + k).wait()
-
-            for rows, u in up_act(h, w[slot, 0], i):
-                for n in range(RANKS):
-                    acc[rows, n * COLS:(n + 1) * COLS] += jnp.dot(
-                        u, w[slot, 1, n].reshape(CHUNK, COLS), preferred_element_type=jnp.float32
-                    )
-
-            rows = rows_of(i)
+                for k in range(PARTS // 2):
+                    load(c * PARTS + k, k).wait()
+
+            def some(g, _):
+                blocks = [i * (TILE // BLOCK) + g * UP_BLOCKS + j for j in range(UP_BLOCKS)]
+                pre = [
+                    jnp.dot(h[block_rows(b), :], wu[...].reshape(DIM, CHUNK), preferred_element_type=jnp.float32)
+                    for b in blocks
+                ]
+                for b, z in zip(blocks, pre):
+                    u[b] = gelu(z).astype(jnp.bfloat16)
+                return 0
+
+            lax.fori_loop(0, TILE // BLOCK // UP_BLOCKS, some, 0)
+
+        def down_phase(c, i):
+            @pl.when(i == 0)
+            def _():
+                for k in range(PARTS // 2, PARTS):
+                    load(c * PARTS + k, k).wait()
+
+            def some(g, _):
+                for j in range(DOWN_BLOCKS):
+                    b = i * (TILE // BLOCK) + g * DOWN_BLOCKS + j
+                    for n in range(RANKS):
+                        acc[block_rows(b), down_cols(n)] += down(u, wd, b, n)
+                return 0
+
+            lax.fori_loop(0, TILE // BLOCK // DOWN_BLOCKS, some, 0)
 
             @pl.when(lax.rem(c, PER_LAYER) == PER_LAYER - 1)
             def _():
-                h[rows, :] = acc[rows, :].astype(jnp.bfloat16)
-                acc[rows, :] = h[rows, :].astype(jnp.float32)
+                lax.fori_loop(0, TILE // BLOCK, lambda j, _: next_h(i * (TILE // BLOCK) + j), 0)
+
+        def next_h(b):
+            h[block_rows(b), :] = acc[block_rows(b), :].astype(jnp.bfloat16)
+            acc[block_rows(b), :] = h[block_rows(b), :].astype(jnp.float32)
+            return 0
+
+        def first_acc(b):
+            acc[block_rows(b), :] = h[block_rows(b), :].astype(jnp.float32)
+            return 0
 
         def step(t, _):
             s = t - AHEAD
@@ -260,11 +282,17 @@
                 def _():
                     x_in.wait()
 
-                acc[rows_of(i), :] = h[rows_of(i), :].astype(jnp.float32)
-
-            @pl.when(s >= 0)
-            def _():
-                compute(s // TILES, lax.rem(s, TILES))
+                lax.fori_loop(0, TILE // BLOCK, lambda j, _: first_acc(i * (TILE // BLOCK) + j), 0)
+
+            c, i = s // (2 * PHASE), lax.rem(s + 2 * PHASE, 2 * PHASE)
+
+            @pl.when((s >= 0) & (i < PHASE))
+            def _():
+                up_phase(c, i)
+
+            @pl.when((s >= 0) & (i >= PHASE))
+            def _():
+                down_phase(c, i - PHASE)
 
             return 0
 
@@ -277,8 +305,8 @@
             return 0
 
         lax.fori_loop(PIECES - RING, PIECES, drain, 0)
-        for k in range(PARTS):
-            load(LAST * PARTS + k).wait()
+        for k in range(PARTS // 2, PARTS):
+            load(LAST * PARTS + k, k).wait()
 
 
 def mlp_stack(lr, lens, w_up, g_up, w_dn, g_dn, x):
@@ -292,16 +320,18 @@
             jax.ShapeDtypeStruct((PIECES - HELD, PART_ROWS, CHUNK), jnp.float32),
             pltpu.VMEM((TOKENS, DIM), jnp.bfloat16),
             pltpu.VMEM((TOKENS, DIM), jnp.float32),
-            pltpu.VMEM((2, 2, RANKS, PARTS // 2, PART_ROWS, CHUNK), jnp.bfloat16),
+            pltpu.VMEM((TOKENS // BLOCK, BLOCK, CHUNK), jnp.bfloat16),
+            pltpu.VMEM((RANKS, PARTS // 2, PART_ROWS, CHUNK), jnp.bfloat16),
+            pltpu.VMEM((RANKS, PARTS // 2, PART_ROWS, COLS), jnp.bfloat16),
         ),
         in_specs=[pl.BlockSpec(memory_space=pltpu.SMEM)] * 2 + [hbm] * 5,
-        out_specs=(hbm, hbm, vmem, vmem, vmem),
+        out_specs=(hbm, hbm) + (vmem,) * 5,
         scratch_shapes=[
             dma((WINDOW,)), dma((PIECES,)),
             dma((RING,)), dma((PIECES,)),
             dma((RING,)), dma((PIECES,)),
             dma((RING,)), dma((PIECES,)),
-            dma((2, PARTS)), dma, dma((STAGES,)), dma((STAGES,)), dma((STAGES,)),
+            dma((PARTS,)), dma, dma((STAGES,)), dma((STAGES,)), dma((STAGES,)),
         ],
         compiler_params=pltpu.CompilerParams(
             collective_id=0, has_side_effects=True, vmem_limit_bytes=STACK_VMEM
@@ -312,21 +342,19 @@
 
 
 def last_kernel(
-    lens, left, h_in, acc_in, w, new_up, new_dn, y_ref, h, acc, zero, zero_sem, held_sem, back_in, back_out, y_sem
+    lens, left, h_in, acc_in, u, wd, new_up, new_dn, y_ref, h, acc, zero,
+    zero_sem, held_sem, back_in, back_out, y_sem,
 ):
-    del h_in, acc_in
+    del h_in
     side = lax.axis_index("side")
 
-    def y_copy(slot, j):
-        rows = pl.ds(pl.multiple_of(j * HALF, HALF), HALF)
-        return pltpu.make_async_copy(
-            h.at[pl.ds(pl.multiple_of(slot * HALF, HALF), HALF)], y_ref.at[0, rows], y_sem
-        )
+    def y_copy(src, b):
+        return pltpu.make_async_copy(h.at[block_rows(src)], y_ref.at[0, block_rows(b)], y_sem)
 
     @pl.when(side == 0)
     def trainer():
         def held_copy(c, k):
-            return pltpu.make_async_copy(held_piece(acc, c, k), piece_of(new_up, new_dn, c, k), held_sem)
+            return pltpu.make_async_copy(held_piece(acc_in, c, k), piece_of(new_up, new_dn, c, k), held_sem)
 
         def each(lo, hi, fn):
             def body(c, _):
@@ -344,12 +372,17 @@
             b = lax.rem(c, BACK // PARTS) * PARTS + k
             return pltpu.make_async_copy(stage(acc, b), piece_of(new_up, new_dn, c, k), back_out.at[b])
 
-        held = HELD // PARTS
+        held, blocks = HELD // PARTS, TOKENS // BLOCK
         each(held, held + BACK // PARTS, lambda c, k: back_read(c, k).start())
-        each(0, held, lambda c, k: held_copy(c, k).start())
-        h[0:HALF, :] = jnp.zeros((HALF, DIM), jnp.bfloat16)
+        h[block_rows(0), :] = jnp.zeros((BLOCK, DIM), jnp.bfloat16)
 
         def bring(c, _):
+            for a in (c - held, c - held + CHUNKS - held):
+                @pl.when(a < held)
+                def _():
+                    for k in range(PARTS):
+                        held_copy(a, k).start()
+
             for k in range(PARTS):
                 back_read(c, k).wait()
                 back_write(c, k).start()
@@ -360,15 +393,18 @@
                     back_write(c - 1, k).wait()
                     back_read(c + 1, k).start()
 
+            for b in (2 * (c - held), 2 * (c - held) + 1):
+                @pl.when(b < blocks)
+                def _():
+                    y_copy(0, b).start()
+
             return 0
 
         lax.fori_loop(held, CHUNKS, bring, 0)
-        for j in range(2 * TILES):
-            y_copy(0, j).start()
         each(0, held, lambda c, k: held_copy(c, k).wait())
         each(CHUNKS - 2, CHUNKS, lambda c, k: back_write(c, k).wait())
-        for j in range(2 * TILES):
-            y_copy(0, j).wait()
+        for b in range(blocks):
+            y_copy(0, b).wait()
 
     @pl.when(side == 1)
     def generator():
@@ -382,44 +418,38 @@
 
             lax.fori_loop(0, CHUNKS, body, 0)
 
+        each_zero(lambda copy: copy.start())
         length = lens[0]
-        slot = LAST % 2
+        per = OUT_TILE // BLOCK
+
+        def send(i):
+            for j in range(per):
+                y_copy(i * per + j, i * per + j).start()
 
         def step(i, _):
-            for k, (rows, u) in enumerate(up_act(h, w[slot, 0], i)):
-                j = 2 * i + k
-                at = lax.broadcasted_iota(jnp.int32, (HALF, COLS), 0) + j * HALF
+            for j in range(per):
+                b = i * per + j
+                at = lax.broadcasted_iota(jnp.int32, (BLOCK, COLS), 0) + b * BLOCK
                 for n in range(RANKS):
-                    cols = slice(n * COLS, (n + 1) * COLS)
-                    total = acc[rows, cols] + jnp.dot(
-                        u, w[slot, 1, n].reshape(CHUNK, COLS), preferred_element_type=jnp.float32
-                    )
-                    h[rows, cols] = jnp.where(at < length, total, 0.0).astype(jnp.bfloat16)
-
-            @pl.when(i == 0)
-            def _():
-                each_zero(lambda copy: copy.start())
-
-            @pl.when(i >= 1)
-            def _():
-                y_copy(2 * i - 2, 2 * i - 2).start()
-                y_copy(2 * i - 1, 2 * i - 1).start()
-
-            return 0
-
-        lax.fori_loop(0, TILES, step, 0)
-        for j in range(2 * TILES - 2, 2 * TILES):
-            y_copy(j, j).start()
+                    total = acc_in[block_rows(b), down_cols(n)] + down(u, wd, b, n)
+                    h[block_rows(b), down_cols(n)] = jnp.where(at < length, total, 0.0).astype(jnp.bfloat16)
+
+            pl.when(i >= 1)(lambda: send(i - 1))
+            return 0
+
+        steps = TOKENS // OUT_TILE
+        lax.fori_loop(0, steps, step, 0)
+        send(steps - 1)
         each_zero(lambda copy: copy.wait())
-        for j in range(2 * TILES):
-            y_copy(j, j).wait()
-
-
-def last_step(lens, left, h, acc, w, up_shape, dn_shape, y_shape):
+        for b in range(TOKENS // BLOCK):
+            y_copy(b, b).wait()
+
+
+def last_step(lens, left, h, acc, u, wd, up_shape, dn_shape, y_shape):
     dma = pltpu.SemaphoreType.DMA
     hbm = pl.BlockSpec(memory_space=pl.ANY)
     vmem = pl.BlockSpec(memory_space=pltpu.VMEM)
-    h, acc, w = (pltpu.with_memory_space_constraint(v, pltpu.VMEM) for v in (h, acc, w))
+    h, acc, u, wd = (pltpu.with_memory_space_constraint(v, pltpu.VMEM) for v in (h, acc, u, wd))
     new_up, new_dn, y, _, _ = pl.pallas_call(
         last_kernel,
         out_shape=(
@@ -429,7 +459,7 @@
             pltpu.VMEM((TOKENS, DIM), jnp.bfloat16),
             pltpu.VMEM((TOKENS, DIM), jnp.float32),
         ),
-        in_specs=[pl.BlockSpec(memory_space=pltpu.SMEM), hbm, vmem, vmem, vmem],
+        in_specs=[pl.BlockSpec(memory_space=pltpu.SMEM), hbm] + [vmem] * 4,
         out_specs=(hbm, hbm, hbm, vmem, vmem),
         input_output_aliases={2: 3, 3: 4},
         scratch_shapes=[
@@ -439,7 +469,7 @@
         compiler_params=pltpu.CompilerParams(vmem_limit_bytes=STACK_VMEM),
         cost_estimate=pl.CostEstimate(flops=18_000_000_000, bytes_accessed=67_000_000, transcendentals=2_000_000),
         name="last",
-    )(lens, left, h, acc, w)
+    )(lens, left, h, acc, u, wd)
     return new_up, new_dn, y
 
 
@@ -449,10 +479,10 @@
     act_spec = P("side", "rep", None)
 
     def device_step(w_up, w_down, g_up, g_down, learn_rate, prompts, prompt_lens):
-        _, left, h, acc, w = mlp_stack(
+        _, left, h, acc, u, _, wd = mlp_stack(
             learn_rate.reshape(1), prompt_lens, w_up, g_up, w_down, g_down, prompts[0]
         )
-        return last_step(prompt_lens, left, h, acc, w, w_up.shape, w_down.shape, prompts.shape)
+        return last_step(prompt_lens, left, h, acc, u, wd, w_up.shape, w_down.shape, prompts.shape)
 
     return jax.shard_map(
         device_step,

time: 591 us -> 589 us (level)
  no operation moved by 1% of the time
where the time goes in v3:
time: 589 us; the launch traced here: 588 us
  Pallas kernels  586 us (99%)
    pallas_call x1, Pallas kernels, mlp_stack(): pl.pallas_call(stack_kernel, out_shape=(jax.ShapeDtypeStruct((PIECES, RAN...  565 us
    pallas_call x1, Pallas kernels, last_step(): pl.pallas_call(last_kernel, out_shape=(jax.ShapeDtypeStruct(up_shape, jnp...  21.2 us

profile of v3, /device:TPU:4, one launch (start us, length us, event | category | flops | bytes accessed | tf_op | source)
XLA Modules:
  0.0 588.1 jit_solution(3170703655935949205)
XLA Ops:
  1.9 565.0 %stack.1 = (bf16[96,4,256,512]{3,2,1,0:T(8,128)(2,1)}, f32[40,256,512]{2,1,0:T(8,128)}, bf16[4096,2048]{1,0:T(8,128)(2,1)S(1)}, f32[4096,2048]{1,0:T(8,128)S(1)}...) custom-call(f32[1]{0:T(128)} %bitcast.2.lr_ref, ...), custom_call_target="tpu_custom_call" | custom-call | flops 399999991808 | bytes 300000000 | tf_op jit(solution)/shard_map/stack/pallas_call | solution.py:316
  566.9 21.2 %last.1 = (f32[1,2,512,6144]{3,2,1,0:T(8,128)}, f32[1,2,6144,512]{3,2,1,0:T(8,128)}, bf16[1,4096,2048]{2,1,0:T(8,128)(2,1)}, bf16[4096,2048]{1,0:T(8,128)(2,1)S(1)}, f32[4096,2048]{1,0:T(8,128)S(1)}) custom-call(s32[1]{0:T(128)S(6)} %copy.15.lens, f32[40,256,512]{2,1,0:T(8,128)} %get-tuple-element.11.left, ...), custom_call_target="tpu_custom_call", output_to_operand_aliasing={{3}: (2, {}), {4}: (3, {})} | custom-call | flops 17999998976 | bytes 67000000 | tf_op jit(solution)/shard_map/last/pallas_call | solution.py:453

commit v4 on v3

--- a/solution.py
+++ b/solution.py
@@ -29,7 +29,8 @@
 HELD = 56
 BACK = 8
 OUT_TILE = 512
-UP_BLOCKS, DOWN_BLOCKS = 4, 4
+BLOCKS = TOKENS // BLOCK
+GROUP = 64
 STACK_VMEM = 8_300_000
 
 
@@ -70,7 +71,7 @@
 
 def stack_kernel(
     lr_ref, lens, w_up, g_up, w_dn, g_dn, x_ref, land, left, h, acc, u, wu, wd,
-    y_send, y_recv, x_send, x_recv, own_send, own_recv, far_send, far_recv,
+    pre, y_send, y_recv, x_send, x_recv, own_send, own_recv, far_send, far_recv,
     w_sem, x_sem, w_in, g_in, left_sem,
 ):
     del lens
@@ -187,6 +188,7 @@
     def generator():
         x_in = pltpu.make_async_copy(x_ref, h, x_sem)
         x_in.start()
+        pre[...] = jnp.zeros_like(pre)
         for to in ((0, rep), (1, pair), (1, cross)):
             pl.semaphore_signal(barrier, inc=1, device_id=to, device_id_type=MESH)
         pl.semaphore_wait(barrier, 3)
@@ -228,32 +230,34 @@
                 for k in range(PARTS // 2):
                     load(c * PARTS + k, k).wait()
 
-            def some(g, _):
-                blocks = [i * (TILE // BLOCK) + g * UP_BLOCKS + j for j in range(UP_BLOCKS)]
-                pre = [
-                    jnp.dot(h[block_rows(b), :], wu[...].reshape(DIM, CHUNK), preferred_element_type=jnp.float32)
-                    for b in blocks
-                ]
-                for b, z in zip(blocks, pre):
-                    u[b] = gelu(z).astype(jnp.bfloat16)
+            for j in range(TILE // BLOCK):
+                b = i * (TILE // BLOCK) + j
+                z = jnp.dot(h[block_rows(b), :], wu[...].reshape(DIM, CHUNK), preferred_element_type=jnp.float32)
+                act_of_pre(lax.rem(b + BLOCKS - 1, BLOCKS))
+                pre[...] = z
+
+        def act_of_pre(b):
+            u[b] = gelu(pre[...]).astype(jnp.bfloat16)
+
+        def last_act():
+            def group(q, _):
+                rows = pl.ds(pl.multiple_of(q * GROUP, GROUP), GROUP)
+                u[BLOCKS - 1, rows, :] = gelu(pre[rows, :]).astype(jnp.bfloat16)
                 return 0
 
-            lax.fori_loop(0, TILE // BLOCK // UP_BLOCKS, some, 0)
+            lax.fori_loop(0, BLOCK // GROUP, group, 0)
 
         def down_phase(c, i):
             @pl.when(i == 0)
             def _():
+                last_act()
                 for k in range(PARTS // 2, PARTS):
                     load(c * PARTS + k, k).wait()
 
-            def some(g, _):
-                for j in range(DOWN_BLOCKS):
-                    b = i * (TILE // BLOCK) + g * DOWN_BLOCKS + j
-                    for n in range(RANKS):
-                        acc[block_rows(b), down_cols(n)] += down(u, wd, b, n)
-                return 0
-
-            lax.fori_loop(0, TILE // BLOCK // DOWN_BLOCKS, some, 0)
+            for j in range(TILE // BLOCK):
+                b = i * (TILE // BLOCK) + j
+                for n in range(RANKS):
+                    acc[block_rows(b), down_cols(n)] += down(u, wd, b, n)
 
             @pl.when(lax.rem(c, PER_LAYER) == PER_LAYER - 1)
             def _():
@@ -297,6 +301,7 @@
             return 0
 
         lax.fori_loop(0, AHEAD + STEPS, step, 0)
+        last_act()
 
         def drain(p, _):
             x_copy(p, rep).wait_send()
@@ -327,6 +332,7 @@
         in_specs=[pl.BlockSpec(memory_space=pltpu.SMEM)] * 2 + [hbm] * 5,
         out_specs=(hbm, hbm) + (vmem,) * 5,
         scratch_shapes=[
+            pltpu.VMEM((BLOCK, CHUNK), jnp.float32),
             dma((WINDOW,)), dma((PIECES,)),
             dma((RING,)), dma((PIECES,)),
             dma((RING,)), dma((PIECES,)),

time: 589 us -> 586 us (level)
  no operation moved by 1% of the time
where the time goes in v4:
time: 586 us
  Pallas kernels  584 us (100%)
    pallas_call x1, Pallas kernels, mlp_stack(): pl.pallas_call(stack_kernel, out_shape=(jax.ShapeDtypeStruct((PIECES, RAN...  563 us
    pallas_call x1, Pallas kernels, last_step(): pl.pallas_call(last_kernel, out_shape=(jax.ShapeDtypeStruct(up_shape, jnp...  21.2 us

profile of v4, /device:TPU:4, one launch (start us, length us, event | category | flops | bytes accessed | tf_op | source)
XLA Modules:
  0.0 585.7 jit_solution(15275561385925184982)
XLA Ops:
  1.9 562.6 %stack.1 = (bf16[96,4,256,512]{3,2,1,0:T(8,128)(2,1)}, f32[40,256,512]{2,1,0:T(8,128)}, bf16[4096,2048]{1,0:T(8,128)(2,1)S(1)}, f32[4096,2048]{1,0:T(8,128)S(1)}...) custom-call(f32[1]{0:T(128)} %bitcast.2.lr_ref, ...), custom_call_target="tpu_custom_call" | custom-call | flops 399999991808 | bytes 300000000 | tf_op jit(solution)/shard_map/stack/pallas_call | solution.py:321
  564.6 21.2 %last.1 = (f32[1,2,512,6144]{3,2,1,0:T(8,128)}, f32[1,2,6144,512]{3,2,1,0:T(8,128)}, bf16[1,4096,2048]{2,1,0:T(8,128)(2,1)}, bf16[4096,2048]{1,0:T(8,128)(2,1)S(1)}, f32[4096,2048]{1,0:T(8,128)S(1)}) custom-call(s32[1]{0:T(128)S(6)} %copy.15.lens, f32[40,256,512]{2,1,0:T(8,128)} %get-tuple-element.11.left, ...), custom_call_target="tpu_custom_call", output_to_operand_aliasing={{3}: (2, {}), {4}: (3, {})} | custom-call | flops 17999998976 | bytes 67000000 | tf_op jit(solution)/shard_map/last/pallas_call | solution.py:459

commit v5 on v4

--- a/solution.py
+++ b/solution.py
@@ -12,7 +12,7 @@
 CHUNK = 512
 CHUNKS = LAYERS * FFN // CHUNK
 PER_LAYER = FFN // CHUNK
-PARTS = 4
+PARTS = 8
 PART_ROWS = 2 * CHUNK // PARTS
 PIECES = CHUNKS * PARTS
 BLOCK = 256
@@ -21,13 +21,13 @@
 PHASE = TILES
 LAST = CHUNKS - 1
 STEPS = LAST * 2 * PHASE + PHASE
-AHEAD, X_LAG, PAIR_LAG = 7, 3, 1
+AHEAD, X_LAG, PAIR_LAG = 7, 2, 1
 PER = 2 * PHASE // PARTS
 WINDOW = 4
 RING = 8
 STAGES = 3
-HELD = 56
-BACK = 8
+HELD = 112
+BACK = 16
 OUT_TILE = 512
 BLOCKS = TOKENS // BLOCK
 GROUP = 64
@@ -47,13 +47,17 @@
     return dn_ref.at[0, layer, pl.ds(first, PART_ROWS), :]
 
 
+ACROSS = DIM // CHUNK
+
+
 def held_piece(acc, c, k):
-    return acc.at[pl.ds(pl.multiple_of(c * PART_ROWS, PART_ROWS), PART_ROWS), pl.ds(k * CHUNK, CHUNK)]
+    first = pl.multiple_of((c * (PARTS // ACROSS) + k // ACROSS) * PART_ROWS, PART_ROWS)
+    return acc.at[pl.ds(first, PART_ROWS), pl.ds(k % ACROSS * CHUNK, CHUNK)]
 
 
 def stage(acc, s):
-    first = pl.multiple_of((HELD + s) // PARTS * PART_ROWS, PART_ROWS)
-    col = pl.multiple_of(lax.rem(s, PARTS) * CHUNK, CHUNK)
+    first = pl.multiple_of((HELD + s) // ACROSS * PART_ROWS, PART_ROWS)
+    col = pl.multiple_of(lax.rem(s, ACROSS) * CHUNK, CHUNK)
     return acc.at[pl.ds(first, PART_ROWS), pl.ds(col, CHUNK)]
 
 
@@ -87,7 +91,7 @@
         )
 
     def y_copy(p):
-        return remote(u.at[lax.rem(p, RING)], p, rep, y_send.at[lax.rem(p, WINDOW)], y_recv.at[p], (1, rep))
+        return remote(u.at[lax.rem(p, RING), pl.ds(0, PART_ROWS)], p, rep, y_send.at[lax.rem(p, WINDOW)], y_recv.at[p], (1, rep))
 
     def x_copy(p, slot):
         return remote(land.at[p, slot], p, slot, x_send.at[lax.rem(p, RING)], x_recv.at[p], (1, cross))
@@ -145,7 +149,7 @@
                     copy.wait()
                 s = lax.rem(p, STAGES)
                 new = w_stage(s)[...] - lr * g_stage(s)[...]
-                u[lax.rem(p, RING)] = new.astype(jnp.bfloat16)
+                u[lax.rem(p, RING), 0:PART_ROWS, :] = new.astype(jnp.bfloat16)
 
                 @pl.when(p < HELD)
                 def _():

time: 586 us -> 588 us (level)
  no operation moved by 1% of the time
where the time goes in v5:
time: 588 us
  Pallas kernels  586 us (100%)
    pallas_call x1, Pallas kernels, mlp_stack(): pl.pallas_call(stack_kernel, out_shape=(jax.ShapeDtypeStruct((PIECES, RAN...  565 us
    pallas_call x1, Pallas kernels, last_step(): pl.pallas_call(last_kernel, out_shape=(jax.ShapeDtypeStruct(up_shape, jnp...  21.2 us

profile of v5, /device:TPU:4, one launch (start us, length us, event | category | flops | bytes accessed | tf_op | source)
XLA Modules:
  0.0 587.7 jit_solution(7981544139306689892)
XLA Ops:
  1.9 564.5 %stack.1 = (bf16[192,4,128,512]{3,2,1,0:T(8,128)(2,1)}, f32[80,128,512]{2,1,0:T(8,128)}, bf16[4096,2048]{1,0:T(8,128)(2,1)S(1)}, f32[4096,2048]{1,0:T(8,128)S(1)...) custom-call(f32[1]{0:T(128)} %bitcast.2.lr_ref, ...), custom_call_target="tpu_custom_call" | custom-call | flops 399999991808 | bytes 300000000 | tf_op jit(solution)/shard_map/stack/pallas_call | solution.py:325
  566.5 21.2 %last.1 = (f32[1,2,512,6144]{3,2,1,0:T(8,128)}, f32[1,2,6144,512]{3,2,1,0:T(8,128)}, bf16[1,4096,2048]{2,1,0:T(8,128)(2,1)}, bf16[4096,2048]{1,0:T(8,128)(2,1)S(1)}, f32[4096,2048]{1,0:T(8,128)S(1)}) custom-call(s32[1]{0:T(128)S(6)} %copy.15.lens, f32[80,128,512]{2,1,0:T(8,128)} %get-tuple-element.11.left, ...), custom_call_target="tpu_custom_call", output_to_operand_aliasing={{3}: (2, {}), {4}: (3, {})} | custom-call | flops 17999998976 | bytes 67000000 | tf_op jit(solution)/shard_map/last/pallas_call | solution.py:463
